TPU v7x, 32 devices: a whole 2x2x4 slice. The times are simulated.
32 devices in a mesh: band: 16 (over z, y, core), sub: 2 (over x).
Axes of the slice: x: 2, y: 2, z: 4, core: 2. Of those that a mesh axis runs over, the one named last changes fastest.
Arguments:
- land_values: bfloat16 [64, 524288], P(None, ('band', 'sub')), may hold values from -6 to 6
- area_weights: bfloat16 [4096, 128, 128], P(('band', 'sub')), may hold values from 0.0019989014 to 0.029907227
- land_mask: int32 [524288], P(('band', 'sub')), may hold values 0 or 1
- dest_band: int32 [4096, 1], P(('band', 'sub')), may hold values from 0 to 15; in each aligned block of 128 rows (0 to 127, 128 to 255, ...) at most 16 rows name the same one
- dest_tile: int32 [4096], P(('band', 'sub')), may hold values from 0 to 399
- ocean_mask: int32 [819200], P(('band', 'sub')), may hold values 0 or 1
Outputs:
- remapped: float32 [64, 819200], P(None, ('band', 'sub'))
Inputs may be any that keep to these rules, and one draw needn't show every extreme that they name: `dest_band`: each device's 128 blocks name any one band at most 16 times; in every draw some device names one band exactly 16 times.
All inputs are finite; a program needn't handle non-finite values. No bound on the sum of `land_mask` or of `ocean_mask` on one device may be relied on, other than what follows from the above.
Results may differ from a plain program's by a relative error of at most 0.005.
Values may be sent and summed in bfloat16 or wider, within the bound.
No kernel may reach another device: no remote copies, remote signals or barrier semaphores. Data moves between devices by JAX's collectives and lax.ppermute only.
A program may use at most 128 MiB of HBM per device.

v0:
```python
import jax
import jax.numpy as jnp
from jax import lax
from jax.sharding import PartitionSpec as P

cover_floor = 0.5


def slot_table(group_key, slot_count, capacity):
    block_order = jnp.arange(group_key.shape[0], dtype=jnp.int32)
    earlier = (group_key[:, None] == group_key[None, :]) & (
        block_order[None, :] < block_order[:, None]
    )
    rank_in = jnp.sum(earlier.astype(jnp.int32), axis=1)
    slot_of = group_key * capacity + rank_in
    return jnp.arange(slot_count, dtype=jnp.int32)[:, None] == slot_of[None, :]


def place_tiles(partial_value, covered, tile_recv, tile_count):
    placing = (tile_recv[:, None] == jnp.arange(tile_count, dtype=jnp.int32)[None, :]).astype(
        jnp.bfloat16
    )
    summed = jnp.einsum("st,sfo->fto", placing, partial_value, preferred_element_type=jnp.float32)
    coverage = jnp.einsum("st,so->to", placing, covered, preferred_element_type=jnp.float32)
    return (summed, coverage)


def per_device(land_values, area_weights, land_mask, dest_band, dest_tile, ocean_mask):
    fields = land_values.shape[0]
    blocks_here = area_weights.shape[0]
    block_cells = area_weights.shape[1]
    tile_cells = area_weights.shape[2]
    band_count = lax.axis_size("band")
    halves = lax.axis_size("sub")
    capacity = max(2, 2 * blocks_here // band_count)
    slot_count = band_count * capacity
    tiles_half = ocean_mask.shape[0] // tile_cells
    tiles_band = tiles_half * halves
    values = land_values.reshape(fields, blocks_here, block_cells)
    masked = (
        area_weights * land_mask.reshape(blocks_here, block_cells).astype(jnp.bfloat16)[:, :, None]
    )
    target = dest_band[:, 0]
    ocean_keep = ocean_mask.reshape(tiles_half, tile_cells).astype(jnp.float32)
    packing = slot_table(target, slot_count, capacity)
    pack_half = packing.astype(jnp.bfloat16)
    tile_sent = jnp.sum(packing.astype(jnp.int32) * dest_tile[None, :], axis=1).reshape(
        band_count, capacity
    )
    partial_local = jnp.einsum(
        "fbl,blo->bfo", values, masked, preferred_element_type=jnp.float32
    ).astype(jnp.bfloat16)
    covered_local = jnp.sum(masked.astype(jnp.float32), axis=1).astype(jnp.bfloat16)
    sent_partial = jnp.einsum(
        "sb,bfo->sfo", pack_half, partial_local, preferred_element_type=jnp.float32
    ).astype(jnp.bfloat16)
    sent_partial = sent_partial.reshape(band_count, capacity, fields, tile_cells)
    sent_covered = jnp.einsum(
        "sb,bo->so", pack_half, covered_local, preferred_element_type=jnp.float32
    ).astype(jnp.bfloat16)
    sent_covered = sent_covered.reshape(band_count, capacity, tile_cells)
    partial_value, covered, tile_recv = (
        lax.all_to_all(sent_partial, "band", split_axis=0, concat_axis=0, tiled=True),
        lax.all_to_all(sent_covered, "band", split_axis=0, concat_axis=0, tiled=True),
        lax.all_to_all(tile_sent, "band", split_axis=0, concat_axis=0, tiled=True),
    )
    summed, coverage = place_tiles(
        partial_value.reshape(slot_count, fields, tile_cells),
        covered.reshape(slot_count, tile_cells),
        tile_recv.reshape(slot_count),
        tiles_band,
    )
    summed, coverage = (
        lax.psum_scatter(summed, "sub", scatter_dimension=1, tiled=True),
        lax.psum_scatter(coverage, "sub", scatter_dimension=0, tiled=True),
    )
    remapped = summed * ocean_keep[None] / jnp.maximum(coverage, cover_floor)[None]
    return remapped.reshape(fields, tiles_half * tile_cells)


def solution(mesh):
    in_specs = (
        P(None, ("band", "sub")),
        P(("band", "sub"), None, None),
        P(("band", "sub")),
        P(("band", "sub"), None),
        P(("band", "sub")),
        P(("band", "sub")),
    )
    out_specs = P(None, ("band", "sub"))
    return jax.shard_map(
        per_device, mesh=mesh, in_specs=in_specs, out_specs=out_specs, check_vma=False
    )
```

profile of v0, /device:TPU:0, one launch (start us, length us, event | category | flops | bytes accessed | tf_op | source)
XLA Modules:
  0.0 313.6 jit_solution(2422943807315207956)
XLA Ops:
  6.5 0.0 copy-start
  6.5 1.0 convert_reduce_fusion
  7.5 0.7 multiply_add_fusion
  8.2 0.8 select_reduce_fusion
  9.0 0.7 all_to_all.13
  9.7 7.4 %all-to-all-start.1 = ((s32[16,1,16]{2,1,0:T(1,128)}), s32[16,1,16]{2,1,0:T(1,128)S(1)}, u32[]{:S(2)}, u32[]{:S(2)}) async-start(s32[16,1,16]{2,1,0:T(1,128)} %all_to_all.13), calls=%async_computation.1 | async-start | bytes 16384 | tf_op jit(solution)/shard_map/all_to_all | solution.py:65
  17.1 0.0 copy-start.1
  17.1 1.0 convert_bitcast_fusion.2
  18.1 4.7 %multiply_reduce_fusion = bf16[128,128]{1,0:T(8,128)(2,1)S(1)} fusion(bf16[128,128,128]{2,1,0:T(8,128)(2,1)} %param.7, bf16[128,128]{1,0:T(8,128)(2,1)S(1)} %convert_bitcast_fusion.2), kind=kLoop, calls=%fused_computation.3 | loop fusion | flops 4177920 | bytes 4259840 | tf_op jit(solution)/shard_map/reduce_sum | solution.py:53
  22.8 0.0 copy-done
  22.8 0.0 copy-done.1
  22.8 4.1 %convert_bitcast_fusion = bf16[128,64,128]{2,1,0:T(8,128)(2,1)} fusion(bf16[128,128,128]{2,1,0:T(8,128)(2,1)S(1)} %copy-done.1, bf16[128,128]{1,0:T(8,128)(2,1)S(1)} %convert_bitcast_fusion.2, bf16[64,16384]{1,0:T(8,128)(2,1)S(1)} %copy-done), kind=kOutput, calls=%fused_computation.10 | convolution fusion | flops 277872640 | bytes 8421376 | tf_op jit(solution)/shard_map/fbl,blo->bfo/dot_general | solution.py:50
  26.9 0.8 convolution_convert_fusion.1
  27.7 0.0 all-to-all-done.1
  27.7 6.0 %all-to-all-start.2 = ((bf16[16,16,128]{2,1,0:T(8,128)(2,1)}), bf16[16,16,128]{2,1,0:T(8,128)(2,1)S(1)}, u32[]{:S(2)}, u32[]{:S(2)}) async-start(bf16[16,16,128]{2,1,0:T(8,128)(2,1)} %bitcast.9), calls=%async_computation.3 | async-start | bytes 131072 | tf_op jit(solution)/shard_map/all_to_all | solution.py:64
  33.7 3.7 %convolution_convert_fusion = bf16[256,64,128]{2,0,1:T(8,128)(2,1)S(1)} fusion(bf16[128,64,128]{2,1,0:T(8,128)(2,1)} %convert_bitcast_fusion, s32[128]{0:T(128)S(1)} %multiply_add_fusion), kind=kOutput, calls=%fused_computation.6 | convolution fusion | flops 539000832 | bytes 6291968 | tf_op jit(solution)/shard_map/sb,bfo->sfo/dot_general | solution.py:54
  37.4 3.1 copy.11
  40.5 0.1 all-to-all-done.2
  40.6 6.0 %all-to-all-start = ((bf16[16,16,64,128]{3,1,2,0:T(8,128)(2,1)}), bf16[16,16,64,128]{3,1,2,0:T(8,128)(2,1)}, u32[]{:S(2)}, u32[]{:S(2)}) async-start(bf16[16,16,64,128]{3,1,2,0:T(8,128)(2,1)} %copy.11), calls=%async_computation | async-start | bytes 8388608 | tf_op jit(solution)/shard_map/all_to_all | solution.py:63
  46.6 0.0 reduce-scatter.7.cloned.1.call-start
  46.6 0.5 broadcast.14
  47.1 0.6 reduce.4
  47.8 0.1 eq.47
  47.9 0.9 fusion.10
  48.8 0.0 reduce-scatter.7.cloned.1.call-update
  48.8 0.0 reduce-scatter.5.cloned.1.call-start
  48.8 75.3 %all-to-all-done = bf16[16,16,64,128]{3,1,2,0:T(8,128)(2,1)} async-done(((bf16[16,16,64,128]{3,1,2,0:T(8,128)(2,1)}), bf16[16,16,64,128]{3,1,2,0:T(8,128)(2,1)}, u32[]{:S(2)}, u32[]{:S(2)}) %all-to-all-start) | async-done | bytes 4194336 | tf_op jit(solution)/shard_map/all_to_all | solution.py:63
  124.1 3.4 %copy.12 = bf16[16,16,64,128]{3,1,0,2:T(8,128)(2,1)S(1)} copy(bf16[16,16,64,128]{3,1,2,0:T(8,128)(2,1)} %all-to-all-done) | data formatting | bytes 8388608 | tf_op jit(solution)/shard_map/all_to_all | solution.py:63
  127.5 6.6 %convolution_bitcast_fusion = f32[64,400,128]{2,1,0:T(8,128)} fusion(bf16[256,64,128]{2,0,1:T(8,128)(2,1)S(1)} %bitcast.38, s32[256]{0:T(256)S(1)} %eq.47), kind=kOutput, calls=%fused_computation | convolution fusion | flops 1677824000 | bytes 17302528 | tf_op jit(solution)/shard_map/st,sfo->fto/dot_general | solution.py:23
  134.1 0.0 copy-start.2
  134.1 0.0 reduce-scatter.5.cloned.1.call-update
  134.1 0.9 copy-done.2
  135.0 0.0 reduce-scatter.7.cloned.1.call-done
  135.0 0.9 broadcast_maximum_fusion
  135.9 163.5 %reduce-scatter.5.cloned.1.call-done = f32[64,200,128]{2,1,0:T(8,128)} async-done(((f32[64,400,128]{2,1,0:T(8,128)}), f32[64,200,128]{2,1,0:T(8,128)}) %reduce-scatter.5.cloned.1.call-update) | async-done | bytes 6553616 | tf_op jit(solution)/shard_map/reduce_scatter | solution.py:74
  299.4 3.4 %multiply_divide_fusion = f32[64,200,128]{2,1,0:T(8,128)S(1)} fusion(f32[64,200,128]{2,1,0:T(8,128)} %reduce-scatter.5.cloned.1.call-done, f32[200,128]{1,0:T(8,128)S(1)} %broadcast_maximum_fusion, f32[200,128]{1,0:T(8,128)S(1)} %convert_bitcast_fusion.1), kind=kLoop, calls=%fused_computation.2 | loop fusion | flops 3276800 | bytes 13312000 | tf_op jit(solution)/shard_map/div | solution.py:77
  302.8 4.0 %copy.24 = f32[8,8,200,128]{3,1,2,0:T(8,128)} copy(f32[8,8,200,128]{3,2,1,0:T(8,128)S(1)} %bitcast.37) | data formatting | bytes 13107200
  (1 shorter events, 0.0 us)
Async XLA Ops:
  6.5 16.2 %copy-start = (bf16[64,16384]{1,0:T(8,128)(2,1)S(1)}, bf16[64,16384]{1,0:T(8,128)(2,1)}, u32[]{:S(2)}) copy-start(bf16[64,16384]{1,0:T(8,128)(2,1)} %param.6) | copy-start | bytes 6291460
  9.7 18.0 %all-to-all-start.1 = ((s32[16,1,16]{2,1,0:T(1,128)}), s32[16,1,16]{2,1,0:T(1,128)S(1)}, u32[]{:S(2)}, u32[]{:S(2)}) async-start(s32[16,1,16]{2,1,0:T(1,128)} %all_to_all.13), calls=%async_computation.1 | async-start | bytes 16384 | tf_op jit(solution)/shard_map/all_to_all | solution.py:65
  17.1 5.7 %copy-start.1 = (bf16[128,128,128]{2,1,0:T(8,128)(2,1)S(1)}, bf16[128,128,128]{2,1,0:T(8,128)(2,1)}, u32[]{:S(2)}) copy-start(bf16[128,128,128]{2,1,0:T(8,128)(2,1)} %param.7) | copy-start | bytes 12582916
  27.7 12.9 %all-to-all-start.2 = ((bf16[16,16,128]{2,1,0:T(8,128)(2,1)}), bf16[16,16,128]{2,1,0:T(8,128)(2,1)S(1)}, u32[]{:S(2)}, u32[]{:S(2)}) async-start(bf16[16,16,128]{2,1,0:T(8,128)(2,1)} %bitcast.9), calls=%async_computation.3 | async-start | bytes 131072 | tf_op jit(solution)/shard_map/all_to_all | solution.py:64
  40.6 83.5 %all-to-all-start = ((bf16[16,16,64,128]{3,1,2,0:T(8,128)(2,1)}), bf16[16,16,64,128]{3,1,2,0:T(8,128)(2,1)}, u32[]{:S(2)}, u32[]{:S(2)}) async-start(bf16[16,16,64,128]{3,1,2,0:T(8,128)(2,1)} %copy.11), calls=%async_computation | async-start | bytes 8388608 | tf_op jit(solution)/shard_map/all_to_all | solution.py:63
  46.6 88.4 %reduce-scatter.7.cloned.1.call-start = ((), (), s32[]{:S(2)}) async-start(), calls=%async_computation.6 | async-start | bytes 307200
  48.8 250.6 %reduce-scatter.5.cloned.1.call-start = ((), (), s32[]{:S(2)}) async-start(), calls=%async_computation.5 | async-start | bytes 19660800 | tf_op jit(solution)/shard_map/reduce_scatter | solution.py:74
  134.1 0.9 copy-start.2
Sparse Core Ops, SparseCore 0:
  49.6 12.3 reduce-scatter.6
  134.2 165.1 reduce-scatter.4
where the time goes:
time: 314 us
  waiting for transfers between devices  239 us (76%)
  starting transfers between devices  19.5 us (6%)
  matrix products  16 us (5%)
  between operations  13.5 us (4%)
  other arithmetic  13 us (4%)
  local copies, waits for them, and re-layouts  12.6 us (4%)
    reduce_scatter x1, waiting for transfers between devices, per_device(): lax.psum_scatter(summed, 'sub', scatter_dimension=1, tiled=True)  164 us
    all_to_all x1, waiting for transfers between devices, per_device(): lax.all_to_all(sent_partial, 'band', split_axis=0, concat_axis=0, tiled=T...  75.3 us
    all_to_all x1, starting transfers between devices, per_device(): lax.all_to_all(tile_sent, 'band', split_axis=0, concat_axis=0, tiled=True)  7.41 us
    dot_general x1, matrix products, place_tiles(): jnp.einsum('st,sfo->fto', placing, partial_value, preferred_element_type=...  6.55 us
  transfers between devices with their start and end apart: 5, of which 3 were waited for; matrix products, arithmetic and copies ran while one was open for 10% of the time, Pallas kernels for 0%

commit v1 on v0

v1 whole, which is shorter than its diff:
```python
import functools

import jax
import jax.numpy as jnp
from jax import lax
from jax.experimental import pallas as pl
from jax.experimental.pallas import tpu as pltpu
from jax.sharding import PartitionSpec as P

cover_floor = 0.5
axes = ("band", "sub")
vmem_bytes = 56 * 1024 * 1024


def round_up(n, m):
    return -(-n // m) * m


def pick_chunk(total, wanted):
    for steps in range(wanted, 0, -1):
        if total % steps == 0:
            return total // steps
    return total


def pack_kernel(group, slots, owner_ref, slot_ref, values_ref, weights_ref, mask_ref, out_ref, cov_ref):
    step = pl.program_id(0)
    fields = values_ref.shape[0]
    cells = weights_ref.shape[1]

    @pl.when(step == 0)
    def _():
        out_ref[...] = jnp.zeros_like(out_ref)
        cov_ref[...] = jnp.zeros_like(cov_ref)

    keep = mask_ref[...].astype(jnp.float32).astype(jnp.bfloat16)
    for j in range(group):
        block = step * group + j
        owner = owner_ref[block]
        slot = slot_ref[block]
        row = keep[j : j + 1, :]
        kept = values_ref[:, j * cells : (j + 1) * cells] * row
        left = jnp.concatenate([kept, jnp.broadcast_to(row, (16, cells))], axis=0)
        both = jnp.dot(left, weights_ref[j], preferred_element_type=jnp.float32)
        out_ref[owner, pl.ds(pl.multiple_of(slot * fields, fields), fields), :] = both[:fields].astype(
            jnp.bfloat16
        )
        cov_ref[owner, pl.ds(slot, 1), :] = both[fields : fields + 1]

    @pl.when(step == pl.num_programs(0) - 1)
    def _():
        out_ref[:, slots * fields :, :] = cov_ref[...].astype(jnp.bfloat16)


def pack(owner, slot, values, weights, mask, n_dev, slots):
    fields = values.shape[0]
    blocks, cells, tile_cells = weights.shape
    group = pick_chunk(blocks, 8)
    rows = slots * fields + round_up(slots, 16)
    return pl.pallas_call(
        functools.partial(pack_kernel, group, slots),
        out_shape=jax.ShapeDtypeStruct((n_dev, rows, tile_cells), jnp.bfloat16),
        grid_spec=pltpu.PrefetchScalarGridSpec(
            num_scalar_prefetch=2,
            grid=(blocks // group,),
            in_specs=[
                pl.BlockSpec((fields, group * cells), lambda i, *_: (0, i)),
                pl.BlockSpec((group, cells, tile_cells), lambda i, *_: (i, 0, 0)),
                pl.BlockSpec((group, cells), lambda i, *_: (i, 0)),
            ],
            out_specs=pl.BlockSpec((n_dev, rows, tile_cells), lambda i, *_: (0, 0, 0)),
            scratch_shapes=[pltpu.VMEM((n_dev, round_up(slots, 16), tile_cells), jnp.float32)],
        ),
        compiler_params=pltpu.CompilerParams(vmem_limit_bytes=vmem_bytes),
        name="pack",
    )(owner, slot, values, weights, mask)


def pick_kernel(count, fields, slots, which_ref, recv_ref, out_ref, cov_in, cov_out):
    cov_in[...] = recv_ref[:, slots * fields :, :].astype(jnp.float32)
    cov_out[...] = jnp.zeros_like(cov_out)

    def one(k, carry):
        at = which_ref[k]
        src = at // slots
        slot = at % slots
        out_ref[pl.ds(pl.multiple_of(k * fields, fields), fields), :] = recv_ref[
            src, pl.ds(pl.multiple_of(slot * fields, fields), fields), :
        ]
        cov_out[pl.ds(k, 1), :] = cov_in[src, pl.ds(slot, 1), :]
        return carry

    lax.fori_loop(0, count, one, 0)
    out_ref[count * fields :, :] = cov_out[...].astype(jnp.bfloat16)


def pick(which, recv, count, fields, slots):
    n_dev, rows, tile_cells = recv.shape
    cov_rows = round_up(count, 16)
    return pl.pallas_call(
        functools.partial(pick_kernel, count, fields, slots),
        out_shape=jax.ShapeDtypeStruct((count * fields + cov_rows, tile_cells), jnp.bfloat16),
        in_specs=[
            pl.BlockSpec(memory_space=pltpu.SMEM),
            pl.BlockSpec(memory_space=pltpu.VMEM),
        ],
        out_specs=pl.BlockSpec(memory_space=pltpu.VMEM),
        scratch_shapes=[
            pltpu.VMEM((n_dev, rows - slots * fields, tile_cells), jnp.float32),
            pltpu.VMEM((cov_rows, tile_cells), jnp.float32),
        ],
        compiler_params=pltpu.CompilerParams(vmem_limit_bytes=vmem_bytes),
        name="pick",
    )(which, recv)


def place_kernel(
    count, slots, chunk, own_ref, late_ref, recv_ref, fix_ref, keep_ref, out_ref, acc, cover, cov_own, cov_fix
):
    step = pl.program_id(0)
    fields = out_ref.shape[0]
    cells = keep_ref.shape[1]
    tiles = keep_ref.shape[0]
    n_dev = recv_ref.shape[0]

    @pl.when(step == 0)
    def _():
        acc[...] = jnp.zeros_like(acc)
        cover[...] = jnp.zeros_like(cover)
        cov_own[...] = recv_ref[:, slots * fields :, :].astype(jnp.float32)
        cov_fix[...] = fix_ref[count * fields :, :].astype(jnp.float32)

        def own(src, carry):
            for k in range(slots):
                tile = own_ref[src * slots + k]
                acc[tile] += recv_ref[src, k * fields : (k + 1) * fields, :].astype(jnp.float32)
                cover[pl.ds(tile, 1), :] += cov_own[src, k : k + 1, :]
            return carry

        lax.fori_loop(0, n_dev, own, 0)

        def late(k, carry):
            tile = late_ref[k]
            acc[tile] += fix_ref[pl.ds(pl.multiple_of(k * fields, fields), fields), :].astype(jnp.float32)
            cover[pl.ds(tile, 1), :] += cov_fix[pl.ds(k, 1), :]
            return carry

        lax.fori_loop(0, count, late, 0)
        total = cover[:tiles, :]
        cover[:tiles, :] = keep_ref[...].astype(jnp.float32) / jnp.maximum(total, cover_floor)

    for j in range(chunk):
        tile = step * chunk + j
        out_ref[:, j * cells : (j + 1) * cells] = acc[tile] * cover[pl.ds(tile, 1), :]


def place(own, late, recv, fix, keep, count, fields, slots):
    n_dev, rows, cells = recv.shape
    tiles = keep.shape[0]
    chunk = pick_chunk(tiles, 8)
    cov_rows = round_up(count, 16)
    return pl.pallas_call(
        functools.partial(place_kernel, count, slots, chunk),
        out_shape=jax.ShapeDtypeStruct((fields, tiles * cells), jnp.float32),
        grid_spec=pltpu.PrefetchScalarGridSpec(
            num_scalar_prefetch=2,
            grid=(tiles // chunk,),
            in_specs=[
                pl.BlockSpec((n_dev, rows, cells), lambda i, *_: (0, 0, 0)),
                pl.BlockSpec(fix.shape, lambda i, *_: (0, 0)),
                pl.BlockSpec((tiles, cells), lambda i, *_: (0, 0)),
            ],
            out_specs=pl.BlockSpec((fields, chunk * cells), lambda i, *_: (0, i)),
            scratch_shapes=[
                pltpu.VMEM((tiles + 1, fields, cells), jnp.float32),
                pltpu.VMEM((round_up(tiles + 1, 8), cells), jnp.float32),
                pltpu.VMEM((n_dev, rows - slots * fields, cells), jnp.float32),
                pltpu.VMEM((cov_rows, cells), jnp.float32),
            ],
        ),
        compiler_params=pltpu.CompilerParams(vmem_limit_bytes=vmem_bytes),
        name="place",
    )(own, late, recv, fix, keep)


def compact(chosen, values, count, empty):
    order = jnp.arange(chosen.shape[0], dtype=jnp.int32)
    earlier = (order[None, :] < order[:, None]) & chosen[None, :]
    rank = jnp.sum(earlier.astype(jnp.int32), axis=1)
    hit = (jnp.arange(count, dtype=jnp.int32)[:, None] == rank[None, :]) & chosen[None, :]
    got = jnp.sum(jnp.where(hit, (values - empty)[None, :], 0), axis=1)
    return got + empty


def per_device(land_values, area_weights, land_mask, dest_band, dest_tile, ocean_mask):
    fields = land_values.shape[0]
    blocks_here, block_cells, tile_cells = area_weights.shape
    band_count = lax.axis_size("band")
    halves = lax.axis_size("sub")
    assert halves == 2
    n_dev = band_count * halves
    capacity = max(2, 2 * blocks_here // band_count)
    slots = -(-capacity // halves)
    n_slots = n_dev * slots
    tiles = ocean_mask.shape[0] // tile_cells
    me = lax.axis_index("sub")

    band = dest_band[:, 0]
    half = (dest_tile >= tiles).astype(jnp.int32)
    key = band * halves + half
    order = jnp.arange(blocks_here, dtype=jnp.int32)
    same = key[:, None] == key[None, :]
    rank = jnp.sum((same & (order[None, :] < order[:, None])).astype(jnp.int32), axis=1)
    other = key + 1 - 2 * half
    other_count = jnp.sum((other[:, None] == key[None, :]).astype(jnp.int32), axis=1)
    spill = rank >= slots
    owner = jnp.where(spill, other, key)
    slot = jnp.where(spill, other_count + rank - slots, rank)
    flat = owner * slots + slot

    placed = jnp.arange(n_slots, dtype=jnp.int32)[:, None] == flat[None, :]
    tile_sent = jnp.sum(jnp.where(placed, dest_tile[None, :] + 1, 0), axis=1) - 1
    tile_sent = tile_sent.reshape(band_count, 1, halves * slots)
    tile_sent = jnp.broadcast_to(tile_sent, (band_count, halves, halves * slots)).reshape(n_dev, halves * slots)
    spilled = (jnp.arange(n_dev, dtype=jnp.int32)[:, None] == owner[None, :]) & spill[None, :]
    spill_count = jnp.sum(spilled.astype(jnp.int32), axis=1)
    table = jnp.concatenate([tile_sent, jnp.broadcast_to(spill_count[None, :], (n_dev, n_dev))], axis=1)
    table = lax.all_to_all(table, axes, split_axis=0, concat_axis=0, tiled=True)

    packed = pack(
        owner, slot, land_values, area_weights, land_mask.reshape(blocks_here, block_cells), n_dev, slots
    )
    recv = lax.all_to_all(packed, axes, split_axis=0, concat_axis=0, tiled=True)

    both = table[:, : halves * slots].reshape(n_dev, halves, slots)
    mine = jnp.where(me == 0, both[:, 0], both[:, 1]).reshape(n_slots)
    theirs = jnp.where(me == 0, both[:, 1], both[:, 0]).reshape(n_slots)
    low = me * tiles
    mine_here = (mine >= low) & (mine < low + tiles)
    own = jnp.where(mine_here, mine - low, tiles)
    away = (mine >= 0) & ~mine_here
    arriving = (theirs >= low) & (theirs < low + tiles)
    most = jnp.max(jnp.sum(table[:, halves * slots :], axis=0))
    keep = ocean_mask.reshape(tiles, tile_cells)
    which = compact(away, jnp.arange(n_slots, dtype=jnp.int32), n_slots, 0)
    late = compact(arriving, theirs - low, n_slots, tiles)

    def finish(count):
        def run(recv, which, late, own, keep):
            fix = pick(which[:count], recv, count, fields, slots)
            fix = lax.ppermute(fix, "sub", [(0, 1), (1, 0)])
            return place(own, late[:count], recv, fix, keep, count, fields, slots)

        return run

    few = min(n_slots, round_up(3 * n_slots // 16, 16))
    return lax.cond(most <= few, finish(few), finish(n_slots), recv, which, late, own, keep)


def solution(mesh):
    in_specs = (
        P(None, axes),
        P(axes, None, None),
        P(axes),
        P(axes, None),
        P(axes),
        P(axes),
    )
    return jax.shard_map(
        per_device, mesh=mesh, in_specs=in_specs, out_specs=P(None, axes), check_vma=False
    )
```

time: 314 us -> 157 us (0.50)
  waiting for transfers between devices: 239 us -> 111 us
  Pallas kernels: 0 us -> 20.4 us
  matrix products: 16 us -> 0 us
  between operations: 13.5 us -> 0.73 us
  other arithmetic: 13 us -> 4.2 us
  local copies, waits for them, and re-layouts: 12.6 us -> 5.67 us
  starting transfers between devices: 19.5 us -> 14.7 us
    reduce_scatter x1 -> x0, waiting for transfers between devices: 164 us -> none  [per_device(): lax.psum_scatter(summed, 'sub', scatter_dimension=1, tiled=True)]
    pallas_call x0 -> x3, Pallas kernels: none -> 20.4 us  [the longest x1 9.62 us: pack(): pl.pallas_call(functools.partial(pack_kernel, group, slots), out_shape=ja...]
    all_to_all x3 -> x2, waiting for transfers between devices: 75.4 us -> 93.7 us  [the longest x1 93.7 us: per_device(): recv = lax.all_to_all(packed, axes, split_axis=0, concat_axis=0, tiled=True)]
    ppermute x0 -> x1, waiting for transfers between devices: none -> 17.5 us  [run(): fix = lax.ppermute(fix, 'sub', [(0, 1), (1, 0)])]
    dot_general x5 -> x0, matrix products: 16 us -> none  [the longest x1 6.55 us: place_tiles(): jnp.einsum('st,sfo->fto', placing, partial_value, preferred_element_type=...]
    all_to_all x3 -> x2, starting transfers between devices: 19.4 us -> 13.3 us  [the longest x1 7.33 us: per_device(): table = lax.all_to_all(table, axes, split_axis=0, concat_axis=0, tiled=True)]
    reduce_sum x3 -> x8, other arithmetic: 6.43 us -> 1.03 us  [the longest x2 0.27 us: compact(): got = jnp.sum(jnp.where(hit, (values - empty)[None, :], 0), axis=1)]
    all_to_all x3 -> x1, local copies, waits for them, and re-layouts: 4.6 us -> 0.08 us  [per_device(): table = lax.all_to_all(table, axes, split_axis=0, concat_axis=0, tiled=True)]
  transfers between devices with their start and end apart: 5 -> 3, of which waited for: 3 -> 2; matrix products, arithmetic and copies ran while one was open for 10% -> 2% of each run, Pallas kernels for 0% -> 6%
where the time goes in v1:
time: 157 us
  waiting for transfers between devices  111 us (71%)
  Pallas kernels  20.4 us (13%)
  starting transfers between devices  14.7 us (9%)
  local copies, waits for them, and re-layouts  5.67 us (4%)
  other arithmetic  4.2 us (3%)
    all_to_all x1, waiting for transfers between devices, per_device(): recv = lax.all_to_all(packed, axes, split_axis=0, concat_axis=0, tiled=True)  93.7 us
    ppermute x1, waiting for transfers between devices, run(): fix = lax.ppermute(fix, 'sub', [(0, 1), (1, 0)])  17.5 us
    pallas_call x1, Pallas kernels, pack(): pl.pallas_call(functools.partial(pack_kernel, group, slots), out_shape=ja...  9.62 us
    all_to_all x1, starting transfers between devices, per_device(): table = lax.all_to_all(table, axes, split_axis=0, concat_axis=0, tiled=True)  7.33 us
    pallas_call x1, Pallas kernels, place(): pl.pallas_call(functools.partial(place_kernel, count, slots, chunk), out_...  6.96 us
    all_to_all x1, starting transfers between devices, per_device(): recv = lax.all_to_all(packed, axes, split_axis=0, concat_axis=0, tiled=True)  5.95 us
    pallas_call x1, Pallas kernels, pick(): pl.pallas_call(functools.partial(pick_kernel, count, fields, slots), out_...  3.82 us
  transfers between devices with their start and end apart: 3, of which 2 were waited for; matrix products, arithmetic and copies ran while one was open for 2% of the time, Pallas kernels for 6%

profile of v1, /device:TPU:0, one launch (start us, length us, event | category | flops | bytes accessed | tf_op | source)
XLA Modules:
  0.0 156.9 jit_solution(2774235596191485057)
XLA Ops:
  0.0 0.7 fusion.7
  0.7 0.2 convert_reduce_fusion.2
  0.9 1.2 multiply_add_fusion
  2.0 0.0 copy-start.4
  2.0 0.1 select_reduce_fusion.2
  2.2 0.1 sub.34
  2.2 0.1 convert_reduce_fusion.4
  2.4 0.1 pad.1.clone
  2.4 0.6 pad_add_fusion
  3.1 7.3 %all-to-all-start = ((s32[32,1,48]{2,1,0:T(1,128)}), s32[32,1,48]{2,1,0:T(1,128)S(1)}, u32[]{:S(2)}, u32[]{:S(2)}) async-start(s32[32,1,48]{2,1,0:T(1,128)} %bitcast.2), calls=%async_computation | async-start | bytes 32768 | tf_op jit(solution)/shard_map/all_to_all | solution.py:228
  10.4 0.0 copy-done.4
  10.4 9.6 %pack.1 = bf16[32,528,128]{2,1,0:T(8,128)(2,1)} custom-call(s32[128]{0:T(128)} %copy-done.4, s32[128]{0:T(128)} %get-tuple-element.43.slot_ref, bf16[64,16384]{1,0:T(8,128)(2,1)} %values_ref.1, bf16[128,128,128]{2,1,0:T(8,128)(2,1)} %weights_ref.1, s32[128,128]{1,0:T(8,128)} %bitcast.22), custom_call_target="tpu_custom_call" | custom-call | tf_op jit(solution)/shard_map/pack/pallas_call | solution.py:60
  20.0 0.0 copy-start.3
  20.0 0.0 all-to-all-done
  20.0 5.9 %all-to-all-start.1 = ((bf16[32,528,128]{2,1,0:T(8,128)(2,1)}), bf16[32,528,128]{2,1,0:T(8,128)(2,1)}, u32[]{:S(2)}, u32[]{:S(2)}) async-start(bf16[32,528,128]{2,1,0:T(8,128)(2,1)} %pack.1), calls=%async_computation.1 | async-start | bytes 8650752 | tf_op jit(solution)/shard_map/all_to_all | solution.py:233
  26.0 0.1 copy.23
  26.1 0.1 slice_reduce_fusion
  26.2 0.7 reduce_max.9
  27.5 0.1 copy.26
  27.6 0.1 and.74
  27.7 0.1 copy.24
  27.8 0.1 reshape.107
  27.9 0.1 copy.27
  28.0 0.1 sub.38
  28.1 0.1 copy.25
  28.1 0.1 select_n.59
  28.2 0.1 convert_reduce_fusion
  28.4 0.1 convert_reduce_fusion.1
  28.5 0.1 select_reduce_fusion.1
  28.6 0.1 select_reduce_fusion
  28.8 93.7 %all-to-all-done.1 = bf16[32,528,128]{2,1,0:T(8,128)(2,1)} async-done(((bf16[32,528,128]{2,1,0:T(8,128)(2,1)}), bf16[32,528,128]{2,1,0:T(8,128)(2,1)}, u32[]{:S(2)}, u32[]{:S(2)}) %all-to-all-start.1) | async-done | bytes 4325408 | tf_op jit(solution)/shard_map/all_to_all | solution.py:233
  122.4 0.0 copy-done.3
  122.4 31.6 %conditional.1 = (f32[64,25600]{1,0:T(8,128)S(1)}) conditional(s32[]{:T(128)} %convert_element_type.25, (s32[256]{0:T(256)S(1)}, bf16[32,528,128]{2,1,0:T(8,128)(2,1)}, s32[256]{0:T(256)S(1)}, s32[256]{0:T(256)S(1)}, s32[200,128]{1,0:T(8,128)S(1)}) %tuple.25, (s32[256]{0:T(256)S(1)}, s32[256]{0:T(256)S(1)}, bf16[32,528,128]{2,1,0:T(8,128)(2,1)}, ...), branch_computations={%region_10.11_spmd, %region_11.12_spmd} | conditional | bytes 34078796 | solution.py:257
  122.4 0.5 slice.5.which_ref
  123.0 3.8 %pick.3 = bf16[3120,128]{1,0:T(8,128)(2,1)} custom-call(s32[48]{0:T(128)} %slice.5.which_ref, bf16[32,528,128]{2,1,0:T(8,128)(2,1)} %get-tuple-element.35.recv_ref), custom_call_target="tpu_custom_call" | custom-call | tf_op jit(solution)/shard_map/cond/branch_1_fun/pick/pallas_call | solution.py:100
  126.8 1.4 collective-permute-start.1
  128.2 0.5 slice.4.late_ref
  128.7 17.5 %collective-permute-done.1.fix_ref = bf16[3120,128]{1,0:T(8,128)(2,1)S(1)} collective-permute-done((bf16[3120,128]{1,0:T(8,128)(2,1)}, bf16[3120,128]{1,0:T(8,128)(2,1)S(1)}, u32[]{:S(2)}, u32[]{:S(2)}) %collective-permute-start.1) | collective-permute-done | bytes 798752 | tf_op jit(solution)/shard_map/cond/branch_1_fun/ppermute | solution.py:251
  146.3 0.0 copy-start.2
  146.3 0.9 copy-done.2
  147.1 7.0 %place.3 = f32[64,25600]{1,0:T(8,128)S(1)} custom-call(s32[256]{0:T(256)S(1)} %get-tuple-element.33.own_ref, s32[48]{0:T(128)} %slice.4.late_ref, bf16[32,528,128]{2,1,0:T(8,128)(2,1)} %get-tuple-element.35.recv_ref, bf16[3120,128]{1,0:T(8,128)(2,1)} %copy-done.2, s32[200,128]{1,0:T(8,128)S(1)} %get-tuple-element.37.keep_ref), custom_call_target="tpu_custom_call" | custom-call | tf_op jit(solution)/shard_map/cond/branch_1_fun/place/pallas_call | solution.py:162
  154.1 0.0 copy-start
  154.1 2.8 %copy-done = f32[64,25600]{1,0:T(8,128)} copy-done((f32[64,25600]{1,0:T(8,128)}, f32[64,25600]{1,0:T(8,128)S(1)}, u32[]{:S(2)}) %copy-start) | copy-done | bytes 6553624
  (7 shorter events, 0.1 us)
Async XLA Ops:
  2.0 8.4 %copy-start.4 = (s32[128]{0:T(128)}, s32[128]{0:T(128)S(1)}, u32[]{:S(2)}) copy-start(s32[128]{0:T(128)S(1)} %get-tuple-element.42.owner_ref) | copy-start | bytes 1540
  3.1 17.0 %all-to-all-start = ((s32[32,1,48]{2,1,0:T(1,128)}), s32[32,1,48]{2,1,0:T(1,128)S(1)}, u32[]{:S(2)}, u32[]{:S(2)}) async-start(s32[32,1,48]{2,1,0:T(1,128)} %bitcast.2), calls=%async_computation | async-start | bytes 32768 | tf_op jit(solution)/shard_map/all_to_all | solution.py:228
  20.0 102.4 %copy-start.3 = (s32[25600]{0:T(1024)S(1)}, s32[25600]{0:T(1024)}, u32[]{:S(2)}) copy-start(s32[25600]{0:T(1024)} %param.13) | copy-start | bytes 307204
  20.0 102.4 %all-to-all-start.1 = ((bf16[32,528,128]{2,1,0:T(8,128)(2,1)}), bf16[32,528,128]{2,1,0:T(8,128)(2,1)}, u32[]{:S(2)}, u32[]{:S(2)}) async-start(bf16[32,528,128]{2,1,0:T(8,128)(2,1)} %pack.1), calls=%async_computation.1 | async-start | bytes 8650752 | tf_op jit(solution)/shard_map/all_to_all | solution.py:233
  126.8 19.5 %collective-permute-start.1 = (bf16[3120,128]{1,0:T(8,128)(2,1)}, bf16[3120,128]{1,0:T(8,128)(2,1)S(1)}, u32[]{:S(2)}, u32[]{:S(2)}) collective-permute-start(bf16[3120,128]{1,0:T(8,128)(2,1)} %pick.3), channel_id=1, source_target_pairs={{0,1},{1,0},{2,3},{3,2},{4,5},{5,4},{6,7},{7,6},{8,9},{9,8},{10,11... | collective-permute-start | bytes 2396168 | tf_op jit(solution)/shard_map/cond/branch_1_fun/ppermute | solution.py:251
  146.3 0.9 copy-start.2
  154.1 2.8 %copy-start = (f32[64,25600]{1,0:T(8,128)}, f32[64,25600]{1,0:T(8,128)S(1)}, u32[]{:S(2)}) copy-start(f32[64,25600]{1,0:T(8,128)S(1)} %get-tuple-element.55) | copy-start | bytes 19660804

commit v2 on v1

v2 whole, which is shorter than its diff:
```python
import functools

import jax
import jax.numpy as jnp
from jax import lax
from jax.experimental import pallas as pl
from jax.experimental.pallas import tpu as pltpu
from jax.sharding import PartitionSpec as P

cover_floor = 0.5
axes = ("band", "sub")
vmem_bytes = 56 * 1024 * 1024


def round_up(n, m):
    return -(-n // m) * m


def pick_chunk(total, wanted):
    for steps in range(wanted, 0, -1):
        if total % steps == 0:
            return total // steps
    return total


def pack_kernel(
    group, slots, owner_ref, slot_ref, values_ref, weights_ref, mask_ref, meta_ref, lead_ref, tail_ref, cov_ref
):
    step = pl.program_id(0)
    fields = values_ref.shape[0]
    cells = weights_ref.shape[1]
    last = tail_ref.shape[1] // slots
    first = fields - last

    @pl.when(step == 0)
    def _():
        lead_ref[...] = jnp.zeros_like(lead_ref)
        tail_ref[...] = jnp.zeros_like(tail_ref)
        cov_ref[...] = jnp.zeros_like(cov_ref)
        cov_ref[:, slots : slots + meta_ref.shape[1], :] = meta_ref[...]

    keep = mask_ref[...].astype(jnp.float32).astype(jnp.bfloat16)
    for j in range(group):
        block = step * group + j
        owner = owner_ref[block]
        slot = slot_ref[block]
        row = keep[j : j + 1, :]
        kept = values_ref[:, j * cells : (j + 1) * cells] * row
        left = jnp.concatenate([kept, jnp.broadcast_to(row, (16, cells))], axis=0)
        both = jnp.dot(left, weights_ref[j], preferred_element_type=jnp.float32)
        lead_ref[owner, pl.ds(pl.multiple_of(slot * first, 16), first), :] = both[:first].astype(jnp.bfloat16)
        tail_ref[owner, pl.ds(pl.multiple_of(slot * last, 16), last), :] = both[first:fields].astype(
            jnp.bfloat16
        )
        cov_ref[owner, pl.ds(slot, 1), :] = both[fields : fields + 1]

    @pl.when(step == pl.num_programs(0) - 1)
    def _():
        lead_ref[:, slots * first :, :] = cov_ref[...].astype(jnp.bfloat16)


def pack(owner, slot, values, weights, mask, meta, slots, last):
    n_dev, meta_rows = meta.shape[:2]
    cov_rows = round_up(slots + meta_rows, 16)
    fields = values.shape[0]
    blocks, cells, tile_cells = weights.shape
    group = pick_chunk(blocks, 8)
    lead = (n_dev, slots * (fields - last) + cov_rows, tile_cells)
    tail = (n_dev, slots * last, tile_cells)
    return pl.pallas_call(
        functools.partial(pack_kernel, group, slots),
        out_shape=(jax.ShapeDtypeStruct(lead, jnp.bfloat16), jax.ShapeDtypeStruct(tail, jnp.bfloat16)),
        grid_spec=pltpu.PrefetchScalarGridSpec(
            num_scalar_prefetch=2,
            grid=(blocks // group,),
            in_specs=[
                pl.BlockSpec((fields, group * cells), lambda i, *_: (0, i)),
                pl.BlockSpec((group, cells, tile_cells), lambda i, *_: (i, 0, 0)),
                pl.BlockSpec((group, cells), lambda i, *_: (i, 0)),
                pl.BlockSpec(meta.shape, lambda i, *_: (0, 0, 0)),
            ],
            out_specs=(
                pl.BlockSpec(lead, lambda i, *_: (0, 0, 0)),
                pl.BlockSpec(tail, lambda i, *_: (0, 0, 0)),
            ),
            scratch_shapes=[pltpu.VMEM((n_dev, cov_rows, tile_cells), jnp.float32)],
        ),
        compiler_params=pltpu.CompilerParams(vmem_limit_bytes=vmem_bytes),
        name="pack",
    )(owner, slot, values, weights, mask, meta)


def pick_kernel(count, fields, slots, which_ref, recv_ref, out_ref, cov_in, cov_out):
    with_cover = recv_ref.shape[1] > slots * fields
    if with_cover:
        cov_in[...] = recv_ref[:, slots * fields :, :].astype(jnp.float32)
        cov_out[...] = jnp.zeros_like(cov_out)

    def one(k, carry):
        at = which_ref[k]
        src = at // slots
        slot = at % slots
        out_ref[pl.ds(pl.multiple_of(k * fields, 16), fields), :] = recv_ref[
            src, pl.ds(pl.multiple_of(slot * fields, 16), fields), :
        ]
        if with_cover:
            cov_out[pl.ds(k, 1), :] = cov_in[src, pl.ds(slot, 1), :]
        return carry

    lax.fori_loop(0, count, one, 0)
    if with_cover:
        out_ref[count * fields :, :] = cov_out[...].astype(jnp.bfloat16)


def pick(which, recv, count, fields, slots):
    n_dev, rows, tile_cells = recv.shape
    cov_rows = round_up(count, 16)
    extra = cov_rows if rows > slots * fields else 0
    return pl.pallas_call(
        functools.partial(pick_kernel, count, fields, slots),
        out_shape=jax.ShapeDtypeStruct((count * fields + extra, tile_cells), jnp.bfloat16),
        in_specs=[
            pl.BlockSpec(memory_space=pltpu.SMEM),
            pl.BlockSpec(memory_space=pltpu.VMEM),
        ],
        out_specs=pl.BlockSpec(memory_space=pltpu.VMEM),
        scratch_shapes=[
            pltpu.VMEM((n_dev, max(8, rows - slots * fields), tile_cells), jnp.float32),
            pltpu.VMEM((cov_rows, tile_cells), jnp.float32),
        ],
        compiler_params=pltpu.CompilerParams(vmem_limit_bytes=vmem_bytes),
        name="pick",
    )(which, recv)


def place_kernel(
    count, slots, chunk, own_ref, late_ref, lead_ref, tail_ref, fix_lead_ref, fix_tail_ref, keep_ref,
    out_ref, acc, cover, cov_own, cov_fix,
):
    step = pl.program_id(0)
    fields = out_ref.shape[0]
    cells = keep_ref.shape[1]
    tiles = keep_ref.shape[0]
    n_dev = lead_ref.shape[0]
    last = tail_ref.shape[1] // slots
    first = fields - last

    @pl.when(step == 0)
    def _():
        acc[...] = jnp.zeros_like(acc)
        cover[...] = jnp.zeros_like(cover)
        cov_own[...] = lead_ref[:, slots * first :, :].astype(jnp.float32)
        cov_fix[...] = fix_lead_ref[count * first :, :].astype(jnp.float32)

        def own(src, carry):
            for k in range(slots):
                tile = own_ref[src * slots + k]
                acc[tile, :first] += lead_ref[src, k * first : (k + 1) * first, :].astype(jnp.float32)
                acc[tile, first:] += tail_ref[src, k * last : (k + 1) * last, :].astype(jnp.float32)
                cover[pl.ds(tile, 1), :] += cov_own[src, k : k + 1, :]
            return carry

        lax.fori_loop(0, n_dev, own, 0)

        def late(k, carry):
            tile = late_ref[k]
            lead = fix_lead_ref[pl.ds(pl.multiple_of(k * first, 16), first), :]
            tail = fix_tail_ref[pl.ds(pl.multiple_of(k * last, 16), last), :]
            acc[tile, :first] += lead.astype(jnp.float32)
            acc[tile, first:] += tail.astype(jnp.float32)
            cover[pl.ds(tile, 1), :] += cov_fix[pl.ds(k, 1), :]
            return carry

        lax.fori_loop(0, count, late, 0)
        total = cover[:tiles, :]
        cover[:tiles, :] = keep_ref[...].astype(jnp.float32) / jnp.maximum(total, cover_floor)

    for j in range(chunk):
        tile = step * chunk + j
        out_ref[:, j * cells : (j + 1) * cells] = acc[tile] * cover[pl.ds(tile, 1), :]


def place(own, late, lead, tail, fix_lead, fix_tail, keep, count, fields, slots):
    n_dev = lead.shape[0]
    tiles, cells = keep.shape
    chunk = pick_chunk(tiles, 8)
    whole = lambda x: pl.BlockSpec(x.shape, lambda i, *_: (0,) * x.ndim)
    return pl.pallas_call(
        functools.partial(place_kernel, count, slots, chunk),
        out_shape=pltpu.HBM((fields, tiles * cells), jnp.float32),
        grid_spec=pltpu.PrefetchScalarGridSpec(
            num_scalar_prefetch=2,
            grid=(tiles // chunk,),
            in_specs=[whole(lead), whole(tail), whole(fix_lead), whole(fix_tail), whole(keep)],
            out_specs=pl.BlockSpec((fields, chunk * cells), lambda i, *_: (0, i)),
            scratch_shapes=[
                pltpu.VMEM((tiles + 1, fields, cells), jnp.float32),
                pltpu.VMEM((round_up(tiles + 1, 8), cells), jnp.float32),
                pltpu.VMEM((n_dev, lead.shape[1] - slots * (fields - tail.shape[1] // slots), cells), jnp.float32),
                pltpu.VMEM((round_up(count, 16), cells), jnp.float32),
            ],
        ),
        compiler_params=pltpu.CompilerParams(vmem_limit_bytes=vmem_bytes),
        name="place",
    )(own, late, lead, tail, fix_lead, fix_tail, keep)


def compact(chosen, values, count, empty):
    order = jnp.arange(chosen.shape[0], dtype=jnp.int32)
    earlier = (order[None, :] < order[:, None]) & chosen[None, :]
    rank = jnp.sum(earlier.astype(jnp.int32), axis=1)
    hit = (jnp.arange(count, dtype=jnp.int32)[:, None] == rank[None, :]) & chosen[None, :]
    got = jnp.sum(jnp.where(hit, (values - empty)[None, :], 0), axis=1)
    return got + empty


def per_device(land_values, area_weights, land_mask, dest_band, dest_tile, ocean_mask):
    fields = land_values.shape[0]
    blocks_here, block_cells, tile_cells = area_weights.shape
    band_count = lax.axis_size("band")
    halves = lax.axis_size("sub")
    assert halves == 2
    n_dev = band_count * halves
    capacity = max(2, 2 * blocks_here // band_count)
    slots = -(-capacity // halves)
    n_slots = n_dev * slots
    tiles = ocean_mask.shape[0] // tile_cells
    me = lax.axis_index("sub")

    band = dest_band[:, 0]
    half = (dest_tile >= tiles).astype(jnp.int32)
    key = band * halves + half
    order = jnp.arange(blocks_here, dtype=jnp.int32)
    same = key[:, None] == key[None, :]
    rank = jnp.sum((same & (order[None, :] < order[:, None])).astype(jnp.int32), axis=1)
    other = key + 1 - 2 * half
    other_count = jnp.sum((other[:, None] == key[None, :]).astype(jnp.int32), axis=1)
    spill = rank >= slots
    owner = jnp.where(spill, other, key)
    slot = jnp.where(spill, other_count + rank - slots, rank)
    flat = owner * slots + slot

    placed = jnp.arange(n_slots, dtype=jnp.int32)[:, None] == flat[None, :]
    tile_sent = jnp.sum(jnp.where(placed, dest_tile[None, :] + 1, 0), axis=1)
    tile_sent = tile_sent.reshape(band_count, 1, halves * slots)
    tile_sent = jnp.broadcast_to(tile_sent, (band_count, halves, halves * slots)).reshape(n_dev, halves * slots)
    spilled = (jnp.arange(n_dev, dtype=jnp.int32)[:, None] == owner[None, :]) & spill[None, :]
    spill_count = jnp.sum(spilled.astype(jnp.int32), axis=1)
    count_rows = round_up(n_dev, tile_cells) // tile_cells
    pad = ((0, 0), (0, tile_cells - halves * slots))
    counts = jnp.pad(spill_count, (0, count_rows * tile_cells - n_dev)).reshape(1, count_rows, tile_cells)
    meta = jnp.concatenate(
        [
            jnp.pad(tile_sent // 128, pad)[:, None, :],
            jnp.pad(tile_sent % 128, pad)[:, None, :],
            jnp.broadcast_to(counts, (n_dev, count_rows, tile_cells)),
        ],
        axis=1,
    ).astype(jnp.float32)

    last = max(16, fields // 64 * 16)
    first = fields - last
    lead, tail = pack(
        owner,
        slot,
        land_values,
        area_weights,
        land_mask.reshape(blocks_here, block_cells),
        meta,
        slots,
        last,
    )
    lead = lax.all_to_all(lead, axes, split_axis=0, concat_axis=0, tiled=True)
    tail, lead = lax.optimization_barrier((tail, lead))
    tail = lax.all_to_all(tail, axes, split_axis=0, concat_axis=0, tiled=True)

    table = lead[:, slots * first + slots : slots * first + slots + 2 + count_rows, :].astype(jnp.int32)
    both = table[:, 0, : halves * slots] * 128 + table[:, 1, : halves * slots] - 1
    both = both.reshape(n_dev, halves, slots)
    mine = jnp.where(me == 0, both[:, 0], both[:, 1]).reshape(n_slots)
    theirs = jnp.where(me == 0, both[:, 1], both[:, 0]).reshape(n_slots)
    low = me * tiles
    mine_here = (mine >= low) & (mine < low + tiles)
    own = jnp.where(mine_here, mine - low, tiles)
    away = (mine >= 0) & ~mine_here
    arriving = (theirs >= low) & (theirs < low + tiles)
    most = jnp.max(jnp.sum(table[:, 2:, :], axis=0))
    keep = ocean_mask.reshape(tiles, tile_cells)
    which = compact(away, jnp.arange(n_slots, dtype=jnp.int32), n_slots, 0)
    late = compact(arriving, theirs - low, n_slots, tiles)

    def hand_over(received, count, width):
        chosen = pick(which[:count], received, count, width, slots)
        return lax.ppermute(chosen, "sub", [(0, 1), (1, 0)])

    few = min(n_slots, round_up(3 * n_slots // 16, 16))
    fix_lead = hand_over(lead, few, first)
    fix_tail = hand_over(tail, few, last)

    def all_fit():
        return place(own, late[:few], lead, tail, fix_lead, fix_tail, keep, few, fields, slots)

    def redo():
        return place(
            own,
            late,
            lead,
            tail,
            hand_over(lead, n_slots, first),
            hand_over(tail, n_slots, last),
            keep,
            n_slots,
            fields,
            slots,
        )

    return lax.cond(most <= few, all_fit, redo)


def solution(mesh):
    in_specs = (
        P(None, axes),
        P(axes, None, None),
        P(axes),
        P(axes, None),
        P(axes),
        P(axes),
    )
    return jax.shard_map(
        per_device, mesh=mesh, in_specs=in_specs, out_specs=P(None, axes), check_vma=False
    )
```

time: 157 us -> 144 us (0.917)
  waiting for transfers between devices: 111 us -> 24.8 us
  blocking collectives: 0 us -> 82.4 us
  starting transfers between devices: 14.7 us -> 6.55 us
  local copies, waits for them, and re-layouts: 5.67 us -> 1.94 us
  Pallas kernels: 20.4 us -> 23.5 us
    all_to_all x0 -> x1, blocking collectives: none -> 82.4 us  [per_device(): lead = lax.all_to_all(lead, axes, split_axis=0, concat_axis=0, tiled=True)]
    all_to_all x2 -> x1, waiting for transfers between devices: 93.7 us -> 19.1 us  [per_device(): tail = lax.all_to_all(tail, axes, split_axis=0, concat_axis=0, tiled=True)]
    ppermute x1 -> x2, waiting for transfers between devices: 17.5 us -> 5.67 us  [hand_over(): return lax.ppermute(chosen, 'sub', [(0, 1), (1, 0)])]
    all_to_all x2 -> x1, starting transfers between devices: 13.3 us -> 3.51 us  [per_device(): tail = lax.all_to_all(tail, axes, split_axis=0, concat_axis=0, tiled=True)]
    unnamed x6 -> x4, local copies, waits for them, and re-layouts: 2.79 us -> 0.01 us
    pallas_call x1, Pallas kernels: 6.96 us -> 8.89 us  [place(): pl.pallas_call(functools.partial(place_kernel, count, slots, chunk), out_...]
    ppermute x1 -> x2, starting transfers between devices: 1.42 us -> 3.04 us  [hand_over(): return lax.ppermute(chosen, 'sub', [(0, 1), (1, 0)])]
    pallas_call x1 -> x2, Pallas kernels: 3.82 us -> 4.77 us  [pick(): pl.pallas_call(functools.partial(pick_kernel, count, fields, slots), out_...]
  transfers between devices with their start and end apart: 3 -> 3, of which waited for: 2 -> 2; matrix products, arithmetic and copies ran while one was open for 2% -> 2% of each run, Pallas kernels for 6% -> 3%
where the time goes in v2:
time: 144 us
  blocking collectives  82.4 us (57%)
  waiting for transfers between devices  24.8 us (17%)
  Pallas kernels  23.5 us (16%)
  starting transfers between devices  6.55 us (5%)
  other arithmetic  4.18 us (3%)
  local copies, waits for them, and re-layouts  1.94 us (1%)
    all_to_all x1, blocking collectives, per_device(): lead = lax.all_to_all(lead, axes, split_axis=0, concat_axis=0, tiled=True)  82.4 us
    all_to_all x1, waiting for transfers between devices, per_device(): tail = lax.all_to_all(tail, axes, split_axis=0, concat_axis=0, tiled=True)  19.1 us
    pallas_call x1, Pallas kernels, pack(): pl.pallas_call(functools.partial(pack_kernel, group, slots), out_shape=(j...  9.81 us
    pallas_call x1, Pallas kernels, place(): pl.pallas_call(functools.partial(place_kernel, count, slots, chunk), out_...  8.89 us
    ppermute x2, waiting for transfers between devices, hand_over(): return lax.ppermute(chosen, 'sub', [(0, 1), (1, 0)])  5.67 us
    pallas_call x2, Pallas kernels, pick(): pl.pallas_call(functools.partial(pick_kernel, count, fields, slots), out_...  4.77 us
    all_to_all x1, starting transfers between devices, per_device(): tail = lax.all_to_all(tail, axes, split_axis=0, concat_axis=0, tiled=True)  3.51 us
    ppermute x2, starting transfers between devices, hand_over(): return lax.ppermute(chosen, 'sub', [(0, 1), (1, 0)])  3.04 us
  transfers between devices with their start and end apart: 3, of which 2 were waited for; matrix products, arithmetic and copies ran while one was open for 2% of the time, Pallas kernels for 3%

profile of v2, /device:TPU:0, one launch (start us, length us, event | category | flops | bytes accessed | tf_op | source)
XLA Modules:
  0.0 144.1 jit_solution(9913362241549941519)
XLA Ops:
  0.0 0.7 fusion.10
  0.7 0.2 convert_reduce_fusion.2
  0.9 1.1 multiply_add_fusion
  2.0 0.0 copy-start.3
  2.0 0.1 select_reduce_fusion.2
  2.1 0.1 broadcast_in_dim.46
  2.3 0.1 convert_reduce_fusion.4
  2.4 0.7 add_convert_fusion.meta_ref
  3.1 0.0 copy-done.3
  3.1 9.8 %pack.1 = (bf16[32,400,128]{2,1,0:T(8,128)(2,1)}, bf16[32,128,128]{2,1,0:T(8,128)(2,1)}) custom-call(s32[128]{0:T(128)} %copy-done.3, s32[128]{0:T(128)} %get-tuple-element.59.slot_ref, bf16[64,16384]{1,0:T(8,128)(2,1)} %values_ref.1, bf16[128,128,128]{2,1,0:T(8,128)(2,1)} %weights_ref.1, s32[128,128]{1,0:T(8,128)} %bitcast.23, ...), custom_call_target="tpu_custom_call" | custom-call | tf_op jit(solution)/shard_map/pack/pallas_call | solution.py:70
  12.9 82.4 %all_to_all.10.recv_ref = bf16[32,400,128]{2,1,0:T(8,128)(2,1)S(1)} all-to-all(bf16[32,400,128]{2,1,0:T(8,128)(2,1)} %get-tuple-element.52), channel_id=1, replica_groups=mesh['band'=16,'sub'=2] {'band','sub'}, dimensions={0} | all-to-all | bytes 6553600 | tf_op jit(solution)/shard_map/all_to_all | solution.py:273
  95.3 0.0 copy-start.2
  95.3 3.5 %all-to-all-start.1 = ((bf16[32,128,128]{2,1,0:T(8,128)(2,1)}), bf16[32,128,128]{2,1,0:T(8,128)(2,1)}, u32[]{:S(2)}, u32[]{:S(2)}) async-start(bf16[32,128,128]{2,1,0:T(8,128)(2,1)} %get-tuple-element.54), calls=%async_computation.1 | async-start | bytes 2097152 | tf_op jit(solution)/shard_map/all_to_all | solution.py:275
  98.8 0.1 slice_reduce_fusion
  98.9 0.6 reduce_max.9
  100.2 0.1 copy.24
  100.3 0.1 copy.27
  100.4 0.1 and.86
  100.5 0.1 copy.25
  100.6 0.1 reshape.108
  100.7 0.1 convert_reduce_fusion.1
  100.8 0.1 select_reduce_fusion.1
  100.9 0.5 slice.33.which_ref
  101.5 2.2 %pick.6 = bf16[2352,128]{1,0:T(8,128)(2,1)} custom-call(s32[48]{0:T(128)} %slice.33.which_ref, bf16[32,400,128]{2,1,0:T(8,128)(2,1)S(1)} %all_to_all.10.recv_ref), custom_call_target="tpu_custom_call" | custom-call | tf_op jit(solution)/shard_map/pick/pallas_call | solution.py:119
  103.7 1.6 %collective-permute-start.2 = (bf16[2352,128]{1,0:T(8,128)(2,1)}, bf16[2352,128]{1,0:T(8,128)(2,1)}, u32[]{:S(2)}, u32[]{:S(2)}) collective-permute-start(bf16[2352,128]{1,0:T(8,128)(2,1)} %pick.6), channel_id=1, source_target_pairs={{0,1},{1,0},{2,3},{3,2},{4,5},{5,4},{6,7},{7,6},{8,9},{9,8},{10,11... | collective-permute-start | bytes 1806344 | tf_op jit(solution)/shard_map/ppermute | solution.py:294
  105.3 0.1 copy.28
  105.4 0.1 sub.45
  105.4 0.1 copy.26
  105.5 0.1 select_n.73
  105.6 0.1 convert_reduce_fusion
  105.7 0.1 select_reduce_fusion
  105.9 19.1 %all-to-all-done.1.recv_ref = bf16[32,128,128]{2,1,0:T(8,128)(2,1)} async-done(((bf16[32,128,128]{2,1,0:T(8,128)(2,1)}), bf16[32,128,128]{2,1,0:T(8,128)(2,1)}, u32[]{:S(2)}, u32[]{:S(2)}) %all-to-all-start.1) | async-done | bytes 1048608 | tf_op jit(solution)/shard_map/all_to_all | solution.py:275
  125.0 2.5 %pick.7 = bf16[768,128]{1,0:T(8,128)(2,1)} custom-call(s32[48]{0:T(128)} %slice.33.which_ref, bf16[32,128,128]{2,1,0:T(8,128)(2,1)} %all-to-all-done.1.recv_ref), custom_call_target="tpu_custom_call" | custom-call | tf_op jit(solution)/shard_map/pick/pallas_call | solution.py:119
  127.5 1.5 %collective-permute-start.3 = (bf16[768,128]{1,0:T(8,128)(2,1)}, bf16[768,128]{1,0:T(8,128)(2,1)S(1)}, u32[]{:S(2)}, u32[]{:S(2)}) collective-permute-start(bf16[768,128]{1,0:T(8,128)(2,1)} %pick.7), channel_id=1, source_target_pairs={{0,1},{1,0},{2,3},{3,2},{4,5},{5,4},{6,7},{7,6},{8,9},{9,8},{10,11... | collective-permute-start | bytes 589832 | tf_op jit(solution)/shard_map/ppermute | solution.py:294
  129.0 0.0 collective-permute-done.2
  129.0 5.7 %collective-permute-done.3 = bf16[768,128]{1,0:T(8,128)(2,1)S(1)} collective-permute-done((bf16[768,128]{1,0:T(8,128)(2,1)}, bf16[768,128]{1,0:T(8,128)(2,1)S(1)}, u32[]{:S(2)}, u32[]{:S(2)}) %collective-permute-start.3) | collective-permute-done | bytes 196640 | tf_op jit(solution)/shard_map/ppermute | solution.py:294
  134.7 0.0 copy-done.2
  134.7 9.4 %conditional.1 = (f32[64,25600]{1,0:T(8,128)}) conditional(s32[]{:T(128)} %convert_element_type.33, (s32[256]{0:T(256)S(1)}, bf16[32,400,128]{2,1,0:T(8,128)(2,1)S(1)}, bf16[32,128,128]{2,1,0:T(8,128)(2,1)}, s32[256]{0:T(256)S(1)}, s32[256]{0:T(256)S(1)}, /*index=5*/s32[200,128]{1,0:T(8,128)S(1)}) %tuple.27, (s32[256]{0:T(256)S(1)}, ...), branch_computations={%region_10.11_spmd, %region_11.12_spmd} | conditional | bytes 34078864 | solution.py:317
  134.7 0.5 slice.5.late_ref
  135.2 8.9 %place.3 = f32[64,25600]{1,0:T(8,128)} custom-call(s32[256]{0:T(256)S(1)} %get-tuple-element.40.own_ref, s32[48]{0:T(128)} %slice.5.late_ref, bf16[32,400,128]{2,1,0:T(8,128)(2,1)S(1)} %get-tuple-element.42.lead_ref, bf16[32,128,128]{2,1,0:T(8,128)(2,1)} %get-tuple-element.43.tail_ref, bf16[2352,128]{1,0:T(8,128)(2,1)} %get-tuple-element.44.fix_lead_ref, ...), custom_call_target="tpu_custom_call" | custom-call | tf_op jit(solution)/shard_map/cond/branch_1_fun/place/pallas_call | solution.py:188
  (12 shorter events, 0.1 us)
Async XLA Ops:
  2.0 1.1 copy-start.3
  95.3 39.4 %copy-start.2 = (s32[25600]{0:T(1024)S(1)}, s32[25600]{0:T(1024)}, u32[]{:S(2)}) copy-start(s32[25600]{0:T(1024)} %param.13) | copy-start | bytes 307204
  95.3 29.7 %all-to-all-start.1 = ((bf16[32,128,128]{2,1,0:T(8,128)(2,1)}), bf16[32,128,128]{2,1,0:T(8,128)(2,1)}, u32[]{:S(2)}, u32[]{:S(2)}) async-start(bf16[32,128,128]{2,1,0:T(8,128)(2,1)} %get-tuple-element.54), calls=%async_computation.1 | async-start | bytes 2097152 | tf_op jit(solution)/shard_map/all_to_all | solution.py:275
  103.7 25.3 %collective-permute-start.2 = (bf16[2352,128]{1,0:T(8,128)(2,1)}, bf16[2352,128]{1,0:T(8,128)(2,1)}, u32[]{:S(2)}, u32[]{:S(2)}) collective-permute-start(bf16[2352,128]{1,0:T(8,128)(2,1)} %pick.6), channel_id=1, source_target_pairs={{0,1},{1,0},{2,3},{3,2},{4,5},{5,4},{6,7},{7,6},{8,9},{9,8},{10,11... | collective-permute-start | bytes 1806344 | tf_op jit(solution)/shard_map/ppermute | solution.py:294
  127.5 7.2 %collective-permute-start.3 = (bf16[768,128]{1,0:T(8,128)(2,1)}, bf16[768,128]{1,0:T(8,128)(2,1)S(1)}, u32[]{:S(2)}, u32[]{:S(2)}) collective-permute-start(bf16[768,128]{1,0:T(8,128)(2,1)} %pick.7), channel_id=1, source_target_pairs={{0,1},{1,0},{2,3},{3,2},{4,5},{5,4},{6,7},{7,6},{8,9},{9,8},{10,11... | collective-permute-start | bytes 589832 | tf_op jit(solution)/shard_map/ppermute | solution.py:294
